TPU v7x, 32 devices: a whole 2x2x4 slice. The times are simulated.
32 devices in a mesh: grp: 2 (over y), img: 4 (over z), dim: 2 (over x), qry: 2 (over core).
Axes of the slice: x: 2, y: 2, z: 4, core: 2. Of those that a mesh axis runs over, the one named last changes fastest.
Arguments:
- caption_vectors: bfloat16 [1024, 1152], P(('grp', 'img', 'qry'), 'dim'), parts along dimension 0, may hold values from -12 to 12
- logit_multiplier: float32 [1024], P(('grp', 'img', 'qry')), parts along dimension 0, may hold values from 0.5 to 8
- picture_vectors: bfloat16 [8192, 1152], P(('grp', 'img'), 'dim'), parts along dimension 0, may hold values from -6 to 6
Outputs:
- lse: float32 [1024], P(('grp', 'img', 'qry')), parts along dimension 0
- top_scores: float32 [1024, 10], P(('grp', 'img', 'qry')), parts along dimension 0
There are 2 independent parts, one for each index of `grp`. A program takes and returns all parts, laid end to end along the dimension named above; each array names one. Nothing has to cross between parts.
All inputs are finite; a program needn't handle non-finite values.
Results may differ from a plain program's by a relative error of at most 0.00073.
Values may be sent and summed in bfloat16 or wider, within the bound.
A program may use at most 64 MiB of HBM per device.

v0:
```python
import functools

import jax
import jax.numpy as jnp
from jax import lax
from jax.experimental import pallas as pl
from jax.experimental.pallas import tpu as pltpu
from jax.sharding import PartitionSpec as P

K = 10
LIST = 16
PAY = 16
LANES = 128
SUB = 8
SPAN = 83.0
TAIL = 16
MESH = pl.DeviceIdType.MESH


def xor_index(a, b, n):
    out, bit = 0, 1
    while bit < n:
        p, q = lax.rem(a // bit, 2), lax.rem(b // bit, 2)
        out = out + bit * (p + q - 2 * p * q)
        bit *= 2
    return out


def exchange(v, i, j):
    hi, lo = jnp.maximum(v[i], v[j]), jnp.minimum(v[i], v[j])
    v[i], v[j] = hi, lo


def sort_desc(v):
    v = list(v)
    n = len(v)
    p = 1
    while p < n:
        k = p
        while k >= 1:
            for j in range(k % p, n - k, 2 * k):
                for i in range(min(k, n - j - k)):
                    if (i + j) // (2 * p) == (i + j + k) // (2 * p):
                        exchange(v, i + j, i + j + k)
            k //= 2
        p *= 2
    return v


def merge_desc(a, b):
    v = [jnp.maximum(a[i], b[LIST - 1 - i]) for i in range(LIST)]
    step = LIST // 2
    while step:
        for i in range(LIST):
            if not i & step:
                exchange(v, i, i + step)
        step //= 2
    return v


def merge_all(lists):
    while len(lists) > 1:
        merged = [merge_desc(lists[i], lists[i + 1]) for i in range(0, len(lists) - 1, 2)]
        lists = merged + lists[len(lists) - len(lists) % 2:]
    return lists[0]


def fold_sublanes(v):
    for shift in (4, 2, 1):
        v = merge_desc(v, [pltpu.roll(x, shift, 0) for x in v])
    return v


def for_each(lo, hi, body):
    if hi - lo <= 4:
        for k in range(lo, hi):
            body(k)
    else:
        lax.fori_loop(lo, hi, lambda k, c: (body(k), c)[1], 0)


def kernel(nd, nz, scale, cap_ref, mult_ref, img_hbm, res_ref,
           img_in, img, qbuf, own, sent, got, pay, fin,
           img_sem, q_send, q_recv, p_send, p_recv, f_send, f_recv):
    x, z = lax.axis_index("dim"), lax.axis_index("img")
    rows = cap_ref.shape[0]
    half = own.shape[1]
    nsrc = nd * nz

    def at_x(j):
        return lax.rem(x + j, nd)

    def at_z(k):
        return xor_index(z, k, nz)

    def columns(j):
        return pl.ds(pl.multiple_of(at_x(j) * (2 * half), 2 * half), 2 * half)

    def load(j):
        return pltpu.make_async_copy(img_hbm.at[:, columns(j)], img_in.at[j], img_sem.at[j])

    for j in list(range(1, nd)) + [0]:
        load(j).start()

    barrier = pltpu.get_barrier_semaphore()

    def greet(n):
        k, j = n // nd, lax.rem(n, nd)
        pl.semaphore_signal(barrier, inc=1, device_id={"dim": at_x(j), "img": at_z(k)}, device_id_type=MESH)

    for_each(1, nsrc, greet)

    r = lax.broadcasted_iota(jnp.int32, (rows, rows), 0)
    c = lax.broadcasted_iota(jnp.int32, (rows, rows), 1)
    mult = jnp.sum(jnp.where(r == c, jnp.broadcast_to(mult_ref[...], (rows, rows)), 0.0), axis=1, keepdims=True)
    width = cap_ref.shape[1]
    pad = (LANES // 2, width)

    def clear(k):
        qbuf[k, : LANES // 2] = jnp.zeros(pad, jnp.bfloat16)
        qbuf[k, LANES:] = jnp.zeros(pad, jnp.bfloat16)

    for_each(0, nz, clear)
    qbuf[0, LANES // 2 : LANES] = (mult * cap_ref[...].astype(jnp.float32) * scale).astype(jnp.bfloat16)
    pl.semaphore_wait(barrier, nsrc - 1)

    def q_copy(k):
        middle = pl.ds(LANES // 2, LANES // 2)
        return pltpu.make_async_remote_copy(
            src_ref=qbuf.at[0, middle], dst_ref=qbuf.at[k, middle],
            send_sem=q_send.at[k], recv_sem=q_recv.at[k],
            device_id={"dim": x, "img": at_z(k)}, device_id_type=MESH)

    def p_copy(k, j):
        return pltpu.make_async_remote_copy(
            src_ref=sent.at[k, j - 1], dst_ref=got.at[k, j - 1],
            send_sem=p_send.at[k, j - 1], recv_sem=p_recv.at[k, j - 1],
            device_id={"dim": at_x(j), "img": z}, device_id_type=MESH)

    def f_copy(k, j):
        return pltpu.make_async_remote_copy(
            src_ref=pay.at[k], dst_ref=fin.at[k * nd + j],
            send_sem=f_send.at[k, j], recv_sem=f_recv.at[k, j],
            device_id={"dim": at_x(j), "img": at_z(k)}, device_id_type=MESH)

    for_each(1, nz, lambda k: q_copy(k).start())

    nt = (((1,), (1,)), ((), ()))

    def partial(k, j):
        first = lax.dot_general(img[j, :half], qbuf[k, LANES // 2 :], nt, preferred_element_type=jnp.float32)
        return first + lax.dot_general(img[j, half:], qbuf[k, :LANES], nt, preferred_element_type=jnp.float32)

    def encode(part, to):
        bound = jnp.maximum(jnp.max(jnp.abs(part), axis=0, keepdims=True) * 1.01, 1e-30).astype(jnp.bfloat16)
        rate = SPAN / bound.astype(jnp.float32)
        to[:half] = jnp.exp(part * rate).astype(jnp.bfloat16)
        to[half:] = jnp.broadcast_to(bound, (TAIL, LANES))

    def turn(j):
        load(j).wait()
        img[j] = img_in[j].T

    def multiply(k, opening=False):
        for j in range(1, nd):
            if opening:
                turn(j)
            encode(partial(k, j), sent.at[k, j - 1])
            p_copy(k, j).start()
        if opening:
            turn(0)
        own[k] = partial(k, 0)

    def select(k):
        for j in range(1, nd):
            p_copy(k, j).wait_recv()
        unit = [got[k, j - 1, half:].astype(jnp.float32)[:SUB] * (1.0 / SPAN) for j in range(1, nd)]
        tiles = []
        for t in range(0, half, 2 * SUB):
            s = own[k, t : t + 2 * SUB]
            code = [jnp.log(got[k, j - 1, t : t + 2 * SUB].astype(jnp.float32)) for j in range(1, nd)]
            for h in range(0, 2 * SUB, SUB):
                v = s[h : h + SUB]
                for j in range(1, nd):
                    v = v + code[j - 1][h : h + SUB] * unit[j - 1]
                tiles.append(v)
        low = jnp.full((SUB, LANES), -jnp.inf, jnp.float32)
        padded = tiles + [low] * (-len(tiles) % LIST)
        lists = [sort_desc(padded[i : i + LIST]) for i in range(0, len(padded), LIST)]
        best = merge_all(lists)
        best = merge_desc(best, [pltpu.roll(v, LANES // 2, 1) for v in best])
        best = fold_sublanes(best)
        sums = [jnp.exp(s - best[0]) for s in tiles]
        while len(sums) > 1:
            sums = [a + b for a, b in zip(sums[::2], sums[1::2])]
        total = jnp.sum(sums[0], axis=0, keepdims=True)
        total = total + pltpu.roll(total, LANES // 2, 1)
        for i in range(K):
            pay[k, i : i + 1] = best[i][:1]
        pay[k, K : K + 1] = total

    def deliver(k, first):
        for j in range(first, nd):
            f_copy(k, j).start()

    def later(k):
        q_copy(k).wait_recv()
        multiply(k)
        if isinstance(k, int) and k == 1:
            finish_first()
        else:
            select(k - 1)
            deliver(k - 1, 0)

    def finish_first():
        select(0)
        fin[0] = pay[0]
        deliver(0, 1)

    pay[...] = jnp.zeros(pay.shape, jnp.float32)
    multiply(0, True)
    if nz > 1:
        later(1)
        for_each(2, nz, later)
        select(nz - 1)
        deliver(nz - 1, 0)
    else:
        finish_first()

    def arrived(n):
        f_copy(n // nd, lax.rem(n, nd)).wait_recv()

    for_each(1, nsrc, arrived)

    low = jnp.full((SUB, LANES), -jnp.inf, jnp.float32)
    lists = []
    for g in range(0, nsrc, SUB):
        lists.append([fin[g : g + SUB, i] for i in range(K)] + [low] * (LIST - K))
    best = fold_sublanes(merge_all([list(v) for v in lists]))
    total = 0.0
    for g in range(0, nsrc, SUB):
        total = total + fin[g : g + SUB, K] * jnp.exp(fin[g : g + SUB, 0] - best[0])
    lse = best[0][:1] + jnp.log(jnp.sum(total, axis=0, keepdims=True))
    res_ref[...] = jnp.concatenate([v[:1] for v in best[:K]] + [lse] + [v[:1] for v in best[K + 1 :]], axis=0)

    for_each(1, nz, lambda k: q_copy(k).wait_send())

    def drained(k):
        for j in range(1, nd):
            p_copy(k, j).wait_send()

    for_each(0, nz, drained)

    def gone(n):
        f_copy(n // nd, lax.rem(n, nd)).wait_send()

    for_each(1, nsrc, gone)


def split_kernel(res_ref, lse_ref, top_ref):
    rows = lse_ref.shape[1]
    top_ref[...] = res_ref[:K, :rows]
    lse_ref[...] = res_ref[K : K + 1, :rows]


def on_device(nd, nz, caption_vectors, logit_multiplier, picture_vectors):
    rows, width = caption_vectors.shape
    images = picture_vectors.shape[0]
    half = images // (2 * nd)
    nsrc = nd * nz
    vmem = pl.BlockSpec(memory_space=pltpu.VMEM)
    f32 = jnp.float32
    res = pl.pallas_call(
        functools.partial(kernel, nd, nz, (width * nd) ** (-0.5)),
        out_shape=jax.ShapeDtypeStruct((LIST, LANES), f32),
        in_specs=[vmem, vmem, pl.BlockSpec(memory_space=pl.ANY)],
        out_specs=vmem,
        scratch_shapes=[
            pltpu.VMEM((nd, width, 2 * half), jnp.bfloat16),
            pltpu.VMEM((nd, 2 * half, width), jnp.bfloat16),
            pltpu.VMEM((nz, LANES + LANES // 2, width), jnp.bfloat16),
            pltpu.VMEM((nz, half, LANES), f32),
            pltpu.VMEM((nz, max(nd - 1, 1), half + TAIL, LANES), jnp.bfloat16),
            pltpu.VMEM((nz, max(nd - 1, 1), half + TAIL, LANES), jnp.bfloat16),
            pltpu.VMEM((nz, PAY, LANES), f32),
            pltpu.VMEM((nsrc, PAY, LANES), f32),
            pltpu.SemaphoreType.DMA((nd,)),
            pltpu.SemaphoreType.DMA((nz,)),
            pltpu.SemaphoreType.DMA((nz,)),
            pltpu.SemaphoreType.DMA((nz, max(nd - 1, 1))),
            pltpu.SemaphoreType.DMA((nz, max(nd - 1, 1))),
            pltpu.SemaphoreType.DMA((nz, nd)),
            pltpu.SemaphoreType.DMA((nz, nd)),
        ],
        compiler_params=pltpu.CompilerParams(collective_id=0, has_side_effects=True),
    )(caption_vectors, logit_multiplier.reshape(1, rows), picture_vectors.T)
    lse, top = pl.pallas_call(
        split_kernel,
        out_shape=(jax.ShapeDtypeStruct((1, rows), f32), jax.ShapeDtypeStruct((K, rows), f32)),
        in_specs=[vmem],
        out_specs=(vmem, vmem),
    )(res)
    return lse.reshape(rows), top.T


def solution(mesh):
    placed = (P(("grp", "img", "qry"), "dim"), P(("grp", "img", "qry")), P(("grp", "img"), "dim"))
    return jax.shard_map(
        functools.partial(on_device, mesh.shape["dim"], mesh.shape["img"]),
        mesh=mesh,
        in_specs=placed,
        out_specs=(P(("grp", "img", "qry")), P(("grp", "img", "qry"), None)),
        check_vma=False,
    )
```

profile of v0, /device:TPU:0, one launch (start us, length us, event | category | flops | bytes accessed | tf_op | source)
XLA Modules:
  0.0 25.6 jit_solution(17548437443613107222)
XLA Ops:
  0.6 23.7 %shard_map.50.res_ref = f32[16,128]{1,0:T(8,128)} custom-call(bf16[64,576]{1,0:T(8,128)(2,1)} %cap_ref.1, f32[1,64]{1,0:T(1,128)} %bitcast.5, bf16[576,1024]{1,0:T(8,128)(2,1)} %bitcast.4), custom_call_target="tpu_custom_call" | custom-call | tf_op jit(solution)/shard_map/pallas_call | solution.py:273
  24.3 1.3 %shard_map.51 = (f32[1,64]{1,0:T(1,128)}, f32[10,64]{1,0:T(8,128)}) custom-call(f32[16,128]{1,0:T(8,128)} %shard_map.50.res_ref), custom_call_target="tpu_custom_call" | custom-call | tf_op jit(solution)/shard_map/pallas_call | solution.py:297
where the time goes:
time: 25.9 us; the launch traced here: 25.6 us
  Pallas kernels  25 us (97%)
  between operations  0.64 us (2%)
    pallas_call x1, Pallas kernels, on_device(): pl.pallas_call(functools.partial(kernel, nd, nz, (width * nd) ** (-0.5)),...  23.7 us
    pallas_call x1, Pallas kernels, on_device(): pl.pallas_call(split_kernel, out_shape=(jax.ShapeDtypeStruct((1, rows), f...  1.3 us

commit v1 on v0

--- a/solution.py
+++ b/solution.py
@@ -79,7 +79,8 @@
         lax.fori_loop(lo, hi, lambda k, c: (body(k), c)[1], 0)
 
 
-def kernel(nd, nz, scale, cap_ref, mult_ref, img_hbm, res_ref,
+def kernel(nd, nz, scale, cap_hbm, mult_hbm, img_hbm, res_ref,
+           cap_ref, mult_ref, in_sem,
            img_in, img, qbuf, own, sent, got, pay, fin,
            img_sem, q_send, q_recv, p_send, p_recv, f_send, f_recv):
     x, z = lax.axis_index("dim"), lax.axis_index("img")
@@ -99,6 +100,10 @@
     def load(j):
         return pltpu.make_async_copy(img_hbm.at[:, columns(j)], img_in.at[j], img_sem.at[j])
 
+    cap_load = pltpu.make_async_copy(cap_hbm, cap_ref, in_sem.at[0])
+    mult_load = pltpu.make_async_copy(mult_hbm, mult_ref, in_sem.at[1])
+    cap_load.start()
+    mult_load.start()
     for j in list(range(1, nd)) + [0]:
         load(j).start()
 
@@ -110,6 +115,8 @@
 
     for_each(1, nsrc, greet)
 
+    mult_load.wait()
+    cap_load.wait()
     r = lax.broadcasted_iota(jnp.int32, (rows, rows), 0)
     c = lax.broadcasted_iota(jnp.int32, (rows, rows), 1)
     mult = jnp.sum(jnp.where(r == c, jnp.broadcast_to(mult_ref[...], (rows, rows)), 0.0), axis=1, keepdims=True)
@@ -272,10 +279,13 @@
     f32 = jnp.float32
     res = pl.pallas_call(
         functools.partial(kernel, nd, nz, (width * nd) ** (-0.5)),
-        out_shape=jax.ShapeDtypeStruct((LIST, LANES), f32),
-        in_specs=[vmem, vmem, pl.BlockSpec(memory_space=pl.ANY)],
+        out_shape=pltpu.VMEM((LIST, LANES), f32),
+        in_specs=[pl.BlockSpec(memory_space=pl.ANY)]*3,
         out_specs=vmem,
         scratch_shapes=[
+            pltpu.VMEM((rows, width), jnp.bfloat16),
+            pltpu.VMEM((1, rows), f32),
+            pltpu.SemaphoreType.DMA((2,)),
             pltpu.VMEM((nd, width, 2 * half), jnp.bfloat16),
             pltpu.VMEM((nd, 2 * half, width), jnp.bfloat16),
             pltpu.VMEM((nz, LANES + LANES // 2, width), jnp.bfloat16),
@@ -299,7 +309,7 @@
         out_shape=(jax.ShapeDtypeStruct((1, rows), f32), jax.ShapeDtypeStruct((K, rows), f32)),
         in_specs=[vmem],
         out_specs=(vmem, vmem),
-    )(res)
+    )(pltpu.with_memory_space_constraint(res, pltpu.VMEM))
     return lse.reshape(rows), top.T
 
 

time: 25.9 us -> 23.9 us (0.923)
  Pallas kernels: 25 us -> 23.1 us
    pallas_call x1, Pallas kernels: 23.7 us -> 22.5 us  [on_device(): pl.pallas_call(functools.partial(kernel, nd, nz, (width * nd) ** (-0.5)),...]
    pallas_call x1, Pallas kernels: 1.3 us -> 0.61 us  [on_device(): pl.pallas_call(split_kernel, out_shape=(jax.ShapeDtypeStruct((1, rows), f...]
where the time goes in v1:
time: 23.9 us; the launch traced here: 23.8 us
  Pallas kernels  23.1 us (97%)
  between operations  0.64 us (3%)
    pallas_call x1, Pallas kernels, on_device(): pl.pallas_call(functools.partial(kernel, nd, nz, (width * nd) ** (-0.5)),...  22.5 us
    pallas_call x1, Pallas kernels, on_device(): pl.pallas_call(split_kernel, out_shape=(jax.ShapeDtypeStruct((1, rows), f...  0.61 us

profile of v1, /device:TPU:0, one launch (start us, length us, event | category | flops | bytes accessed | tf_op | source)
XLA Modules:
  0.0 23.8 jit_solution(7456637064757267344)
XLA Ops:
  0.6 22.5 %shard_map.50.res_ref = f32[16,128]{1,0:T(8,128)S(1)} custom-call(bf16[64,576]{1,0:T(8,128)(2,1)} %cap_hbm.1, f32[1,64]{1,0:T(1,128)} %bitcast.5, bf16[576,1024]{1,0:T(8,128)(2,1)} %bitcast.4), custom_call_target="tpu_custom_call" | custom-call | tf_op jit(solution)/shard_map/pallas_call | solution.py:280
  23.2 0.6 %shard_map.51 = (f32[1,64]{1,0:T(1,128)}, f32[10,64]{1,0:T(8,128)}) custom-call(f32[16,128]{1,0:T(8,128)S(1)} %shard_map.50.res_ref), custom_call_target="tpu_custom_call" | custom-call | tf_op jit(solution)/shard_map/pallas_call | solution.py:307
